TPU v7x, 128 devices: a whole 4x4x4 slice. The times are simulated.
128 devices in a mesh: rep: 1, data: 16 (over z, y), expert: 8 (over x, core).
Axes of the slice: x: 4, y: 4, z: 4, core: 2. Of those that a mesh axis runs over, the one named last changes fastest.
Arguments:
- x: bfloat16 [65536, 2048], P(('rep', 'expert', 'data'))
- expert_idx: int32 [65536, 2], P(('rep', 'expert', 'data'))
- gate: float32 [65536, 2], P(('rep', 'expert', 'data'))
- w_gate: bfloat16 [8, 2048, 5632], P('expert', 'data')
- w_up: bfloat16 [8, 2048, 5632], P('expert', 'data')
- w_down: bfloat16 [8, 5632, 2048], P('expert', None, 'data')
Outputs:
- output: bfloat16 [65536, 2048], P(('rep', 'expert', 'data'))
All inputs are finite; a program needn't handle non-finite values.
Results may differ from a plain program's by a relative error of at most 0.001.
Values are sent between devices in bfloat16 or wider.
A program may use at most 1 GiB of HBM per device.

v0:
```python
import jax
import jax.numpy as jnp
from jax import lax
from jax.sharding import PartitionSpec as P


def capacity_rows(tok_rows, top_k, n_exp):
    return max(8, ((5 * top_k * tok_rows) // (4 * n_exp) + 7) // 8 * 8)


def slot_table(ids_flat, n_exp, n_group, capacity):
    n_local = n_exp // n_group
    one_hot = (ids_flat[:, None] == jnp.arange(n_exp, dtype=jnp.int32)[None, :]).astype(jnp.int32)
    slot_ids = jnp.sum((jnp.cumsum(one_hot, axis=0) - one_hot) * one_hot, axis=1)
    row_base = (ids_flat % n_local) * (n_group * capacity) + (ids_flat // n_local) * capacity
    return jnp.where(slot_ids < capacity, row_base + slot_ids, n_exp * capacity)


def dispatch_rows(x_loc, dest_row, n_slots, top_k):
    tok_rows = x_loc.shape[0]
    pair_token = jnp.arange(dest_row.shape[0], dtype=jnp.int32) // top_k
    src_tok = jnp.full((n_slots,), tok_rows, jnp.int32).at[dest_row].set(pair_token, mode="drop")
    return jnp.take(x_loc, src_tok, axis=0, mode="fill", fill_value=0)


def combine_rows(x_loc, gate_loc, back_rows, dest_row):
    tok_rows, d_model = x_loc.shape
    pair_out = jnp.take(back_rows, dest_row, axis=0, mode="fill", fill_value=0)
    mixed = jnp.sum(pair_out.reshape(tok_rows, gate_loc.shape[1], d_model) * gate_loc[:, :, None], axis=1)
    return (x_loc.astype(jnp.float32) + mixed).astype(jnp.bfloat16)


def expert_ffn(expert_rows, w_gate, w_up, w_down):
    gate_act = jnp.einsum("erd,edf->erf", expert_rows, w_gate, preferred_element_type=jnp.float32)
    up_act = jnp.einsum("erd,edf->erf", expert_rows, w_up, preferred_element_type=jnp.float32)
    hidden = (jax.nn.silu(gate_act) * up_act).astype(jnp.bfloat16)
    return jnp.einsum("erf,efd->erd", hidden, w_down, preferred_element_type=jnp.float32).astype(jnp.bfloat16)


def solution(mesh):
    n_group = mesh.shape["expert"]
    tok_spec = P(("rep", "expert", "data"), None)
    wide_spec = P("expert", "data", None)
    down_spec = P("expert", None, "data")

    def device_step(x_loc, idx_loc, gate_loc, wg_loc, wu_loc, wd_loc):
        tok_rows, d_model = x_loc.shape
        top_k = idx_loc.shape[1]
        n_local = wg_loc.shape[0]
        n_exp = n_local * n_group
        capacity = capacity_rows(tok_rows, top_k, n_exp)
        dest_row = slot_table(idx_loc.reshape(tok_rows * top_k), n_exp, n_group, capacity)
        send_rows = dispatch_rows(x_loc, dest_row, n_exp * capacity, top_k).reshape(n_local, n_group, capacity, d_model)
        recv_rows = lax.all_to_all(send_rows, "expert", 1, 1, tiled=True)
        wg_full = lax.all_gather(wg_loc, "data", axis=1, tiled=True)
        wu_full = lax.all_gather(wu_loc, "data", axis=1, tiled=True)
        wd_full = lax.all_gather(wd_loc, "data", axis=2, tiled=True)
        out_rows = expert_ffn(recv_rows.reshape(n_local, n_group * capacity, d_model), wg_full, wu_full, wd_full)
        back_rows = lax.all_to_all(out_rows.reshape(n_local, n_group, capacity, d_model), "expert", 1, 1, tiled=True)
        return combine_rows(x_loc, gate_loc, back_rows.reshape(n_exp * capacity, d_model), dest_row)

    return jax.shard_map(device_step, mesh=mesh, in_specs=(tok_spec, tok_spec, tok_spec, wide_spec, wide_spec, down_spec), out_specs=tok_spec, check_vma=False)
```

profile of v0, /device:TPU:1, one launch (start us, length us, event | category | flops | bytes accessed | tf_op | source)
XLA Modules:
  0.0 605.2 jit_solution(11667364037664055396)
XLA Ops:
  6.5 0.0 copy-start
  6.5 0.0 all-gather.4.cloned.1.call-start
  6.5 0.7 all-gather.4.cloned.1.call-update
  7.3 0.0 all-gather.6.cloned.1.call-start
  7.3 0.7 all-gather.6.cloned.1.call-update
  8.0 0.0 all-gather.8.cloned.1.call-start
  8.1 0.7 all-gather.8.cloned.1.call-update
  8.7 0.8 copy.13
  9.6 0.0 copy-start.2
  9.6 0.2 eq.31
  9.8 0.2 eq.27
  9.9 2.3 reduce-window.6
  12.2 0.3 slice_reduce_fusion
  12.5 0.2 reduce-window.9
  12.7 0.2 mul.44
  12.9 0.1 add_bitcast_fusion
  13.0 0.0 copy-start.4
  13.0 0.6 copy-done.4
  13.6 0.0 copy-start.6
  13.6 4.3 scatter_custom_fusion
  17.9 0.1 broadcast_in_dim.34
  18.0 0.0 copy-done
  18.0 6.1 %gather_fusion = bf16[1280,2048]{1,0:T(8,128)(2,1)} fusion(bf16[512,2048]{1,0:T(8,128)(2,1)S(1)} %copy-done, s32[2048]{0:T(1024)S(1)} %pad_clamp_fusion), kind=kCustom, calls=%fused_computation | custom fusion | bytes 10490880 | tf_op jit(solution)/shard_map/jit(_take)/gather | solution.py:23
  24.1 0.0 copy-done.2
  24.1 0.0 copy-done.6
  24.1 2.9 broadcast_select_fusion.1
  27.0 65.5 %all_to_all.10 = bf16[1,8,160,2048]{3,2,0,1:T(8,128)(2,1)} all-to-all(bf16[1,8,160,2048]{3,2,0,1:T(8,128)(2,1)S(1)} %broadcast_select_fusion.1), channel_id=1, replica_groups=mesh['rep'=1,'data'=16,'expert'=8] {'expert'}, dimensions={1} | all-to-all | bytes 10485760 | tf_op jit(solution)/shard_map/all_to_all | solution.py:54
  92.5 63.4 %all-gather.4.cloned.1.call-done = bf16[1,2048,5632]{2,1,0:T(8,128)(2,1)} async-done(((bf16[1,128,5632]{2,1,0:T(8,128)(2,1)}), bf16[1,2048,5632]{2,1,0:T(8,128)(2,1)}) %all-gather.4.cloned.1.call-update) | async-done | bytes 23068688 | tf_op jit(solution)/shard_map/all_gather | solution.py:55
  156.0 38.5 %fusion.3 = f32[1280,5632]{1,0:T(8,128)} fusion(bf16[1280,2048]{1,0:T(8,128)(2,1)} %bitcast.54, bf16[1,2048,5632]{2,1,0:T(8,128)(2,1)} %all-gather.4.cloned.1.call-done), kind=kOutput, calls=%fused_computation.7 | convolution fusion | flops 29527900160 | bytes 57147392 | tf_op jit(solution)/shard_map/erd,edf->erf/dot_general | solution.py:34
  194.4 106.7 %all-gather.6.cloned.1.call-done = bf16[1,2048,5632]{2,1,0:T(8,128)(2,1)} async-done(((bf16[1,128,5632]{2,1,0:T(8,128)(2,1)}), bf16[1,2048,5632]{2,1,0:T(8,128)(2,1)}) %all-gather.6.cloned.1.call-update) | async-done | bytes 23068688 | tf_op jit(solution)/shard_map/all_gather | solution.py:56
  301.2 43.3 %multiply_convert_fusion.clone.4 = bf16[1280,5632]{1,0:T(8,128)(2,1)} fusion(f32[1280,5632]{1,0:T(8,128)} %fusion.3, bf16[1280,2048]{1,0:T(8,128)(2,1)} %bitcast.55, bf16[1,2048,5632]{2,1,0:T(8,128)(2,1)} %all-gather.6.cloned.1.call-done), kind=kOutput, calls=%fused_computation.3.clone.clone.clone.1 | convolution fusion | flops 29571153920 | bytes 71565312 | tf_op jit(solution)/shard_map/erd,edf->erf/dot_general | solution.py:35
  344.5 108.4 %all-gather.8.cloned.1.call-done = bf16[1,5632,2048]{2,1,0:T(8,128)(2,1)} async-done(((bf16[1,5632,128]{2,1,0:T(8,128)(2,1)}), bf16[1,5632,2048]{2,1,0:T(8,128)(2,1)}) %all-gather.8.cloned.1.call-update) | async-done | bytes 23068688 | tf_op jit(solution)/shard_map/all_gather | solution.py:57
  452.8 38.5 %fusion.5 = bf16[1280,2048]{1,0:T(8,128)(2,1)} fusion(bf16[1,5632,2048]{2,1,0:T(8,128)(2,1)} %all-gather.8.cloned.1.call-done, bf16[1280,5632]{1,0:T(8,128)(2,1)} %multiply_convert_fusion.clone.4), kind=kOutput, calls=%fused_computation.11 | convolution fusion | flops 29530521600 | bytes 42729472 | tf_op jit(solution)/shard_map/erf,efd->erd/dot_general | solution.py:37
  491.3 0.0 copy-start.5
  491.3 0.0 copy-start.8
  491.3 0.0 copy-start.7
  491.4 0.0 copy-start.3
  491.4 6.7 %all-to-all-start.1 = ((bf16[1,8,160,2048]{3,2,0,1:T(8,128)(2,1)}), bf16[1,8,160,2048]{3,2,0,1:T(8,128)(2,1)}, u32[]{:S(2)}, u32[]{:S(2)}) async-start(bf16[1,8,160,2048]{3,2,0,1:T(8,128)(2,1)} %bitcast.53), calls=%async_computation.1 | async-start | bytes 10485760 | tf_op jit(solution)/shard_map/all_to_all | solution.py:59
  498.1 0.0 copy-done.5
  498.1 0.2 reduce_sum.23
  498.3 0.0 copy-done.8
  498.3 0.1 copy.18
  498.5 0.0 copy-done.7
  498.5 0.0 copy-done.3
  498.5 0.1 compare_and_fusion
  498.6 59.3 %all-to-all-done.1 = bf16[1,8,160,2048]{3,2,0,1:T(8,128)(2,1)} async-done(((bf16[1,8,160,2048]{3,2,0,1:T(8,128)(2,1)}), bf16[1,8,160,2048]{3,2,0,1:T(8,128)(2,1)}, u32[]{:S(2)}, u32[]{:S(2)}) %all-to-all-start.1) | async-done | bytes 5242912 | tf_op jit(solution)/shard_map/all_to_all | solution.py:59
  557.9 12.0 %gather_fusion.1 = bf16[1024,2048]{1,0:T(8,128)(2,1)} fusion(bf16[1280,2048]{1,0:T(8,128)(2,1)} %bitcast.11, s32[1024]{0:T(1024)S(1)} %broadcast_clamp_fusion), kind=kCustom, calls=%fused_computation.1 | custom fusion | bytes 8392704 | tf_op jit(solution)/shard_map/jit(_take)/gather | solution.py:28
  570.0 7.6 %gather.15 = bf16[512,2,2048]{2,1,0:T(2,128)(2,1)} reshape(bf16[1024,2048]{1,0:T(8,128)(2,1)} %gather_fusion.1) | data formatting | bytes 8388608 | tf_op jit(solution)/shard_map/jit(_take)/gather | solution.py:28
  577.6 0.0 copy-start.1
  577.6 19.0 %multiply_reduce_fusion = f32[512,2048]{1,0:T(8,128)S(1)} fusion(bf16[512,2,2048]{2,1,0:T(2,128)(2,1)} %gather.15, pred[512,2]{1,0:T(8,128)(4,1)S(1)} %compare_and_fusion, f32[512,2]{1,0:T(8,128)S(1)} %copy.18), kind=kLoop, calls=%fused_computation.9 | loop fusion | flops 7340032 | bytes 8393728 | tf_op jit(solution)/shard_map/reduce_sum | solution.py:29
  596.6 0.0 copy-done.1
  596.6 2.1 add_convert_fusion
  (9 shorter events, 0.1 us)
Async XLA Ops:
  6.5 11.5 %copy-start = (bf16[512,2048]{1,0:T(8,128)(2,1)S(1)}, bf16[512,2048]{1,0:T(8,128)(2,1)}, u32[]{:S(2)}) copy-start(bf16[512,2048]{1,0:T(8,128)(2,1)} %param.6) | copy-start | bytes 6291460
  6.5 149.4 %all-gather.4.cloned.1.call-start = ((), (), s32[]{:S(2)}) async-start(), calls=%async_computation.2 | async-start | bytes 24510464 | tf_op jit(solution)/shard_map/all_gather | solution.py:55
  7.3 293.9 %all-gather.6.cloned.1.call-start = ((), (), s32[]{:S(2)}) async-start(), calls=%async_computation.3 | async-start | bytes 24510464 | tf_op jit(solution)/shard_map/all_gather | solution.py:56
  8.0 444.8 %all-gather.8.cloned.1.call-start = ((), (), s32[]{:S(2)}) async-start(), calls=%async_computation.4 | async-start | bytes 24510464 | tf_op jit(solution)/shard_map/all_gather | solution.py:57
  9.6 14.5 %copy-start.2 = (s32[512,2]{1,0:T(8,128)}, s32[512,2]{1,0:T(8,128)S(1)}, u32[]{:S(2)}) copy-start(s32[512,2]{1,0:T(8,128)S(1)} %copy.13) | copy-start | bytes 12292
  13.0 0.6 copy-start.4
  13.6 10.6 %copy-start.6 = (s32[1024,1]{0,1:T(1,128)}, s32[1024,1]{0,1:T(1,128)S(1)}, u32[]{:S(2)}) copy-start(s32[1024,1]{0,1:T(1,128)S(1)} %compare_select_fusion.1) | copy-start | bytes 12292
  491.3 6.8 %copy-start.5 = (s32[1024]{0:T(1024)S(1)}, s32[1024]{0:T(1024)}, u32[]{:S(2)}) copy-start(s32[1024]{0:T(1024)} %copy-done.4) | copy-start | bytes 12292
  491.3 7.0 %copy-start.8 = (f32[512,2]{0,1:T(2,128)S(1)}, f32[512,2]{0,1:T(2,128)}, u32[]{:S(2)}) copy-start(f32[512,2]{0,1:T(2,128)} %param.8) | copy-start | bytes 12292
  491.3 7.1 %copy-start.7 = (s32[1024,1]{0,1:T(1,128)S(1)}, s32[1024,1]{0,1:T(1,128)}, u32[]{:S(2)}) copy-start(s32[1024,1]{0,1:T(1,128)} %copy-done.6) | copy-start | bytes 12292
  491.4 7.1 %copy-start.3 = (s32[512,2]{1,0:T(8,128)S(1)}, s32[512,2]{1,0:T(8,128)}, u32[]{:S(2)}) copy-start(s32[512,2]{1,0:T(8,128)} %copy-done.2) | copy-start | bytes 12292
  491.4 66.6 %all-to-all-start.1 = ((bf16[1,8,160,2048]{3,2,0,1:T(8,128)(2,1)}), bf16[1,8,160,2048]{3,2,0,1:T(8,128)(2,1)}, u32[]{:S(2)}, u32[]{:S(2)}) async-start(bf16[1,8,160,2048]{3,2,0,1:T(8,128)(2,1)} %bitcast.53), calls=%async_computation.1 | async-start | bytes 10485760 | tf_op jit(solution)/shard_map/all_to_all | solution.py:59
  577.6 19.0 %copy-start.1 = (bf16[512,2048]{1,0:T(8,128)(2,1)S(1)}, bf16[512,2048]{1,0:T(8,128)(2,1)}, u32[]{:S(2)}) copy-start(bf16[512,2048]{1,0:T(8,128)(2,1)} %param.6) | copy-start | bytes 6291460
Sparse Core Ops, SparseCore 0:
  9.5 146.4 all-gather.3
  158.1 143.0 all-gather.5
  303.3 149.4 all-gather.7
where the time goes:
time: 606 us; the launch traced here: 605 us
  waiting for transfers between devices  340 us (56%)
  matrix products  120 us (20%)
  blocking collectives  65.5 us (11%)
  local copies, waits for them, and re-layouts  32.7 us (5%)
  other arithmetic  26.7 us (4%)
  between operations  13.3 us (2%)
  starting transfers between devices  6.81 us (1%)
    all_gather x1, waiting for transfers between devices, device_step(): wd_full = lax.all_gather(wd_loc, 'data', axis=2, tiled=True)  108 us
    all_gather x1, waiting for transfers between devices, device_step(): wu_full = lax.all_gather(wu_loc, 'data', axis=1, tiled=True)  107 us
    all_to_all x1, blocking collectives, device_step(): recv_rows = lax.all_to_all(send_rows, 'expert', 1, 1, tiled=True)  65.5 us
    all_gather x1, waiting for transfers between devices, device_step(): wg_full = lax.all_gather(wg_loc, 'data', axis=1, tiled=True)  63.4 us
    all_to_all x1, waiting for transfers between devices, device_step(): lax.all_to_all(out_rows.reshape(n_local, n_group, capacity, d_model), 'ex...  59.3 us
    dot_general x1, matrix products, expert_ffn(): jnp.einsum('erd,edf->erf', expert_rows, w_up, preferred_element_type=jnp....  43.3 us
    dot_general x1, matrix products, expert_ffn(): jnp.einsum('erf,efd->erd', hidden, w_down, preferred_element_type=jnp.flo...  38.5 us
    dot_general x1, matrix products, expert_ffn(): jnp.einsum('erd,edf->erf', expert_rows, w_gate, preferred_element_type=jn...  38.5 us
  transfers between devices with their start and end apart: 4, of which 4 were waited for; matrix products, arithmetic and copies ran while one was open for 16% of the time, Pallas kernels for 0%

commit v1 on v0

v1 whole, which is shorter than its diff:
```python
import jax
import jax.numpy as jnp
from jax import lax
from jax.experimental import pallas as pl
from jax.experimental.pallas import tpu as pltpu
from jax.sharding import PartitionSpec as P

MESH = pl.DeviceIdType.MESH
F32 = jnp.float32
BF16 = jnp.bfloat16

T = 512
D = 2048
FF = 5632
FH = FF // 2
E = 8
C = 160
ROWS = 16 * C
FC = 256
NCH = FH // FC
MT = 640
NT = ROWS // MT
PAIR = range(2)
WA = 3072
WB = FF - WA
WBH = WB // 2
FIRST = 8
TICKS = NCH + 4


def al(v):
    return pl.multiple_of(v, 128)


def ynat(s, yl, o):
    return 2 * s + yl if o == 0 else 3 - (2 * s + yl)


def kernel(x_ref, idx_ref, gate_ref, wg_ref, wu_ref, wd_ref,
           y_ref, gu_ref, wdn_ref, back_ref,
           X, H, gv, dv, S, slot_ref, gw_ref,
           own_sem, ownsend_sem, loc_sem, nbr_recv, nbr_send, gu_recv, gu_send,
           wd0_recv, wd0_send, wd_recv, wd_send, tok_recv, tok_send, fwd_recv, fwd_send,
           h_recv, h_send, gl_sem, dl_sem, c_recv, c_send, bl_sem):
    p = lax.axis_index("expert")
    q = lax.axis_index("data")
    x = p // 2
    c = p % 2
    z = q // 4
    y = q % 4
    s = y // 2
    yl = y % 2
    e_own = 2 * x + s
    zm = (z + 3) % 4
    zp = (z + 1) % 4
    zo = (z + 2) % 4
    oc = dict(data=q, expert=2 * x + 1 - c)
    yp = dict(data=z * 4 + 2 * s + 1 - yl, expert=p)
    zpd = dict(data=zp * 4 + y, expert=p)
    zmd = dict(data=zm * 4 + y, expert=p)
    qc = z * 4 + 3 - y
    home = c == s
    b_own = 4 * x + c

    def remote(src, dst, ss, rs, dev):
        return pltpu.make_async_remote_copy(src_ref=src, dst_ref=dst, send_sem=ss, recv_sem=rs,
                                            device_id=dev, device_id_type=MESH)

    def half(i):
        return pl.ds(al(i * FH), FH)

    barrier = pltpu.get_barrier_semaphore()
    for dev in (yp, zpd, zmd):
        pl.semaphore_signal(barrier, inc=1, device_id=dev, device_id_type=MESH)

    def greet(b, _):
        od = (b // 2) % 2
        yd = od * (3 - y) + (1 - od) * y

        @pl.when(b != b_own)
        def _():
            pl.semaphore_signal(barrier, inc=1, device_id=dict(data=z * 4 + yd, expert=2 * (b // 4) + b % 2), device_id_type=MESH)
        return 0

    lax.fori_loop(0, 16, greet, 0)
    pl.semaphore_wait(barrier, 18)

    hx = pl.ds(al(c * FH), FH)
    my_rows = pl.ds(al((z * 4 + yl * 2) * 128), 128)

    def own_copy(m):
        src = (wg_ref, wu_ref)[m]
        return remote(src.at[0, :, half(1 - c)], gu_ref.at[m, my_rows, :], ownsend_sem.at[m], own_sem.at[m], oc)

    def bounce_in(m):
        src = (wg_ref, wu_ref)[m]
        return pltpu.make_async_copy(src.at[0, :, hx], H.at[pl.ds(m * 128, 128), hx], loc_sem.at[m])

    def bounce_out(m):
        return pltpu.make_async_copy(H.at[pl.ds(m * 128, 128), hx], gu_ref.at[m, my_rows, :], own_sem.at[m])

    def nbr_copy(f, h, m):
        src = (wg_ref, wu_ref)[m]
        cols = pl.ds(al(h * FH + f * FC), FC)
        dcols = pl.ds(al(f * FC), FC)
        nyl = (3 - y) % 2
        rows = pl.ds(al((z * 4 + nyl * 2 + 1) * 128), 128)
        return remote(src.at[0, :, cols], gu_ref.at[m, rows, dcols], nbr_send.at[f, h, m], nbr_recv.at[f, m],
                      dict(data=qc, expert=2 * x + h))

    def nbr_start(f):
        @pl.when(jnp.logical_not(home))
        def _():
            for h in PAIR:
                for m in PAIR:
                    nbr_copy(f, h, m).start()

    PARTS = ((WA, WB), (0, WA))

    def wd0_own(i):
        o, n = PARTS[i]
        return remote(wd_ref.at[0, pl.ds(o, n), :], wdn_ref.at[z, yl, pl.ds(o, n), :],
                      wd0_send.at[i], wd0_recv.at[i], oc)

    def wd0_nbr(i):
        o, n = PARTS[i]
        return remote(wd_ref.at[0, pl.ds(o, n), :], wdn_ref.at[z, (3 - y) % 2, pl.ds(o, n), :],
                      wd0_send.at[i], wd0_recv.at[i], dict(data=qc, expert=2 * x + 1))

    def wd0_loc(i):
        o, n = PARTS[i]
        return pltpu.make_async_copy(dv.at[0, pl.ds(o, n), pl.ds(0, 128)], wdn_ref.at[z, yl, pl.ds(o, n), :], wd0_recv.at[i])

    wd_in = pltpu.make_async_copy(wd_ref.at[0], dv.at[0, :, pl.ds(0, 128)], loc_sem.at[2])

    @pl.when(home)
    def _():
        for m in PAIR:
            own_copy(m).start()
            bounce_in(m).start()

        @pl.when(c == 0)
        def _():
            wd_in.start()

        for m in PAIR:
            bounce_in(m).wait()
            bounce_out(m).start()

        @pl.when(c == 0)
        def _():
            wd_in.wait()
            for i in PAIR:
                wd0_loc(i).start()

        @pl.when(c == 1)
        def _():
            for i in PAIR:
                wd0_own(i).start()

    for f in range(3):
        nbr_start(f)

    def rows(zz, l, o, n):
        return pl.ds(al((zz * 4 + l * 2 + o) * 128), n * 128)

    def guc(f, r, i, dev):
        ref = gu_ref.at[:, r, pl.ds(al(f * FC), FC)]
        return remote(ref, ref, gu_send.at[f, i], gu_recv.at[f, i], dev)

    SENT_A = ((z, yl, 0, 2, yp), (z, 0, 0, 4, zpd), (z, 0, 0, 4, zmd), (zm, 0, 0, 2, zpd), (zp, 1, 0, 2, zmd))
    GOT_A = ((z, 1 - yl, 0, 2), (zm, 0, 0, 4), (zp, 0, 0, 4), (zo, 0, 0, 2), (zo, 1, 0, 2))
    SENT_B = ((z, yl, 0, 2, zpd), (z, yl, 0, 2, zmd), (zm, yl, 0, 1, zpd), (zp, yl, 1, 1, zmd),
              (z, yl, 0, 2, yp), (zm, yl, 0, 2, yp), (zp, yl, 0, 2, yp), (zo, yl, 0, 2, yp))
    GOT_B = ((zm, yl, 0, 2), (zp, yl, 0, 2), (zo, yl, 0, 1), (zo, yl, 1, 1),
             (z, 1 - yl, 0, 2), (zm, 1 - yl, 0, 2), (zp, 1 - yl, 0, 2), (zo, 1 - yl, 0, 2))

    def gu_put(f, sent, *ids):
        for i in ids:
            guc(f, rows(*sent[i][:4]), i, sent[i][4]).start()

    def gu_got(f, table, *ids):
        for i in ids:
            guc(f, rows(*table[i]), i, yp).wait_recv()

    def by_tree(f, do_a, do_b):
        pl.when(f % 2 == 0)(do_a)
        pl.when(f % 2 == 1)(do_b)

    def stage1(f):
        for m in PAIR:
            nbr_copy(f, 0, m).wait_recv()

        def do_a():
            gu_put(f, SENT_A, 0)

        def do_b():
            gu_put(f, SENT_B, 0, 1, 4)

        by_tree(f, do_a, do_b)

    def stage2(f):
        def do_a():
            gu_got(f, GOT_A, 0)
            gu_put(f, SENT_A, 1, 2)

        def do_b():
            gu_got(f, GOT_B, 0)
            gu_put(f, SENT_B, 2, 5)
            gu_got(f, GOT_B, 1)
            gu_put(f, SENT_B, 3, 6)

        by_tree(f, do_a, do_b)

    def stage3(f):
        def do_a():
            gu_got(f, GOT_A, 1)
            gu_put(f, SENT_A, 3)
            gu_got(f, GOT_A, 2)
            gu_put(f, SENT_A, 4)

        def do_b():
            gu_got(f, GOT_B, 2, 3)
            gu_put(f, SENT_B, 7)

        by_tree(f, do_a, do_b)

    def stage4(f):
        def do_a():
            gu_got(f, GOT_A, 3, 4)

        def do_b():
            gu_got(f, GOT_B, 4, 5, 6, 7)

        by_tree(f, do_a, do_b)

    def guc_sends(f):
        def wait(sent):
            for i, t in enumerate(sent):
                guc(f, rows(*t[:4]), i, t[4]).wait_send()

        by_tree(f, lambda: wait(SENT_A), lambda: wait(SENT_B))

    def wdc(zz, l, o, n, i, dev):
        ref = wdn_ref.at[zz, l, pl.ds(o, n), :]
        return remote(ref, ref, wd_send.at[i], wd_recv.at[i], dev)

    A = (0, WA)
    B = (WA, WB)
    B0 = (WA, WBH)
    B1 = (WA + WBH, WBH)
    SENT = ((z, yl, *B, 0, zpd), (z, yl, *B, 1, zmd), (z, yl, *B, 2, yp),
            (z, yl, *A, 3, yp), (z, yl, *A, 4, zpd), (z, yl, *A, 5, zmd),
            (z, 1 - yl, *A, 6, zpd), (z, 1 - yl, *A, 7, zmd),
            (zm, yl, *B0, 8, zpd), (zp, yl, *B1, 9, zmd),
            (zm, yl, *B, 10, yp), (zp, yl, *B, 11, yp),
            (zm, 0, *A, 12, zpd), (zp, 1, *A, 13, zmd),
            (zo, yl, *B, 14, yp))
    GOT = ((zm, yl, *B, 0, zpd), (zp, yl, *B, 1, zmd), (z, 1 - yl, *B, 2, yp),
           (z, 1 - yl, *A, 3, yp), (zm, yl, *A, 4, zpd), (zp, yl, *A, 5, zmd),
           (zm, 1 - yl, *A, 6, zpd), (zp, 1 - yl, *A, 7, zmd),
           (zo, yl, *B0, 8, zpd), (zo, yl, *B1, 9, zmd),
           (zm, 1 - yl, *B, 10, yp), (zp, 1 - yl, *B, 11, yp),
           (zo, 0, *A, 12, zpd), (zo, 1, *A, 13, zmd),
           (zo, 1 - yl, *B, 14, yp))

    def put(*ids):
        for i in ids:
            wdc(*SENT[i]).start()

    def got(*ids):
        for i in ids:
            wdc(*GOT[i]).wait_recv()

    lanes = lax.broadcasted_iota(jnp.int32, (T, 128), 1)
    ids = jnp.transpose(idx_ref[...])
    gates = jnp.transpose(gate_ref[...])
    i0 = ids[:, 0:1]
    i1 = ids[:, 1:2]
    hit0 = i0 == lanes
    hit1 = i1 == lanes
    took = jnp.logical_or(hit0, hit1)
    took_f = jnp.where(took, 1.0, 0.0)
    lower = (lax.broadcasted_iota(jnp.int32, (T, T), 0) > lax.broadcasted_iota(jnp.int32, (T, T), 1))
    lower_f = jnp.where(lower, 1.0, 0.0).astype(BF16)
    count = jnp.dot(lower_f, took_f.astype(BF16), preferred_element_type=F32)
    slot_ref[...] = jnp.where(took, count, -1.0).astype(jnp.int32)
    gw_ref[...] = jnp.where(hit0, gates[:, 0:1], 0.0) + jnp.where(hit1, gates[:, 1:2], 0.0)

    def pick(e, r0, n):
        pos = lax.broadcasted_iota(jnp.int32, (n, C), 1)
        return jnp.where(slot_ref[pl.ds(r0, n), e:e + 1] == pos, 1.0, 0.0).astype(BF16)

    def tok_copy(e):
        xe, se = e // 2, e % 2
        same = jnp.where(s == se, 1, 0)
        yd = same * y + (1 - same) * (3 - y)
        o = 1 - same
        b = (x * 2 + o) * 2 + c
        return remote(S.at[e], X.at[pl.ds(pl.multiple_of(b * C, C), C), :],
                      tok_send.at[e], tok_recv.at[x * 2 + o], dict(data=z * 4 + yd, expert=2 * xe + c))

    for e in range(E):
        sel = pick(e, 0, T)
        for zz in range(4):
            r = lax.dot_general(sel, x_ref[:, zz * 512:(zz + 1) * 512], (((0,), (0,)), ((), ())),
                                preferred_element_type=F32).astype(BF16)
            for l in PAIR:
                for o in PAIR:
                    k = zz * 4 + l * 2 + o
                    n = ynat(e % 2, l, o)
                    S[e, :, k * 128:(k + 1) * 128] = r[:, n * 128:(n + 1) * 128]

    def mine(b):
        return pl.ds(pl.multiple_of(b * C, C), C)

    X[mine(b_own), :] = S[e_own]

    def fwd(j, k):
        ref = X.at[mine(j * 2 + k), :]
        return remote(ref, ref, fwd_send.at[j], fwd_recv.at[j], oc)

    def take_tokens(o):
        for j in range(o, 8, 2):
            @pl.when(j != x * 2)
            def _():
                pltpu.make_async_copy(S.at[0], X.at[mine(j * 2 + c), :], tok_recv.at[j]).wait()
            fwd(j, c).start()

    def gu_load(f):
        return pltpu.make_async_copy(gu_ref.at[:, :, pl.ds(al(f * FC), FC)], gv.at[f % 2], gl_sem.at[f % 2])

    def gu_compute(f):
        k = f % 2
        cols = pl.ds(al(c * FH + f * FC), FC)

        def tile(r, _):
            rr = pl.ds(pl.multiple_of(r * MT, MT), MT)
            g = jnp.dot(X[rr, :], gv[k, 0], preferred_element_type=F32)
            u = jnp.dot(X[rr, :], gv[k, 1], preferred_element_type=F32)
            H[rr, cols] = (jax.nn.silu(g) * u).astype(BF16)
            return 0

        lax.fori_loop(0, NT, tile, 0)

    def h_copy(f, k):
        ref = H.at[:, pl.ds(al(k * FH + f * FC), FC)]
        return remote(ref, ref, h_send.at[f], h_recv.at[f], oc)

    def one_chunk(j):
        @pl.when(jnp.logical_or(j == 0, j >= FIRST))
        def _():
            gu_load(j).start()

        @pl.when(j + 1 < FIRST)
        def _():
            gu_load(j + 1).start()

        gu_load(j).wait()
        gu_compute(j)

        @pl.when(j > 0)
        def _():
            h_copy(j - 1, c).start()

    def done_by(i):
        return jnp.where(i < FIRST, 0, jnp.minimum(2 * (i - FIRST + 1), i - 3))

    def during(i, lo, hi, fn):
        pl.when(jnp.logical_and(i >= lo, i < hi))(fn)

    def tick(i, _):
        @pl.when(i == 0)
        def _():
            for m in PAIR:
                own_copy(m).wait_recv()

        during(i, 0, NCH, lambda: stage1(i))
        during(i, 0, E - 1, lambda: tok_copy((e_own + 1 + i) % E).start())
        during(i, 0, NCH - 3, lambda: nbr_start(i + 3))

        @pl.when(jnp.logical_and(i == NCH - 3, jnp.logical_not(home)))
        def _():
            for k in PAIR:
                wd0_nbr(k).start()

        during(i, 2, NCH + 2, lambda: stage3(i - 2))
        during(i, 1, NCH + 1, lambda: stage2(i - 1))

        @pl.when(i == NCH)
        def _():
            wd0_nbr(0).wait_recv()
            put(0, 1, 2)

        @pl.when(i == NCH + 1)
        def _():
            wd0_nbr(1).wait_recv()
            put(3, 4, 5)

        @pl.when(i == NCH + 2)
        def _():
            got(0)
            put(8, 10)
            got(1)
            put(9, 11)

        @pl.when(i == NCH + 3)
        def _():
            got(3)
            put(6, 7)

        during(i, 4, NCH + 4, lambda: stage4(i - 4))

        @pl.when(i == FIRST - 3)
        def _():
            take_tokens(0)

        @pl.when(i == FIRST)
        def _():
            take_tokens(1)
            for j in range(8):
                fwd(j, 1 - c).wait_recv()

        def chunk(j, _):
            one_chunk(j)
            return 0

        lax.fori_loop(done_by(i - 1), done_by(i), chunk, 0)
        return 0

    lax.fori_loop(0, TICKS, tick, 0)
    h_copy(NCH - 1, c).start()

    def d_load(g, zz):
        out = []
        for l in PAIR:
            lane = pl.ds(al(((l + c) % 2) * 128), 128)
            out.append(pltpu.make_async_copy(wdn_ref.at[zz, l], dv.at[g % 2, :, lane], dl_sem.at[g % 2, l]))
        return out

    def place(zz):
        w = c * (1 - s) + (1 - c) * s
        return pl.ds(al(zz * 512 + w * 256), 256)

    def out_copy(g, zz, b):
        xd = b // 4
        cd = b % 2
        od = (b // 2) % 2
        yd = od * (3 - y) + (1 - od) * y
        return remote(X.at[mine(b), pl.ds(g * 256, 256)], back_ref.at[e_own, :, place(zz)],
                      c_send.at[g], c_recv.at[g], dict(data=z * 4 + yd, expert=2 * xd + cd))

    def out_send(g, zz, r):
        for k in range(4):
            b = r * 4 + k

            @pl.when(b != b_own)
            def _():
                out_copy(g, zz, b).start()

    def out_compute(g, zz):
        for d in d_load(g, zz):
            d.wait()

        def tile(r, _):
            rr = pl.ds(pl.multiple_of(r * MT, MT), MT)
            X[rr, g * 256:(g + 1) * 256] = jnp.dot(H[rr, :], dv[g % 2], preferred_element_type=F32).astype(BF16)

            @pl.when(r > 0)
            def _():
                out_send(g, zz, r - 1)
            return 0

        lax.fori_loop(0, NT, tile, 0)
        out_send(g, zz, NT - 1)
        pltpu.make_async_copy(X.at[mine(b_own), pl.ds(g * 256, 256)], back_ref.at[e_own, :, place(zz)], c_recv.at[g]).start()

    def got_all(g):
        pltpu.make_async_copy(X.at[:, pl.ds(0, 256)], X.at[:, pl.ds(0, 256)], c_recv.at[g]).wait()

    def sent_all(g):
        pltpu.make_async_copy(X.at[pl.ds(0, 15 * C), pl.ds(0, 256)], X.at[pl.ds(0, 15 * C), pl.ds(0, 256)], c_send.at[g]).wait()

    def finish(g, zz):
        got_all(g)
        cols = pl.ds(al(zz * 512), 512)
        back = pltpu.make_async_copy(back_ref.at[:, :, cols], S.at[:, :, cols], bl_sem.at[0])
        back.start()
        back.wait()

        def tile(t, _):
            rr = pl.ds(pl.multiple_of(t * 256, 256), 256)
            acc = x_ref[rr, cols].astype(F32)
            for e in range(E):
                part = jnp.dot(pick(e, pl.multiple_of(t * 256, 256), 256), S[e, :, cols], preferred_element_type=F32)
                acc = acc + gw_ref[rr, e:e + 1] * part
            y_ref[rr, cols] = acc.astype(BF16)
            return 0

        lax.fori_loop(0, 2, tile, 0)

    for j in range(8):
        fwd(j, c).wait_send()
    for e in range(E):
        @pl.when(e != e_own)
        def _():
            tok_copy(e).wait_send()

    got(2)
    for d in d_load(0, z):
        d.start()
    for f in range(NCH):
        h_copy(f, 1 - c).wait_recv()
    out_compute(0, z)
    got(8, 9)
    put(14)
    got(4, 5, 6, 7)
    put(12, 13)
    got(10)
    for d in d_load(1, zm):
        d.start()
    got(11)
    out_compute(1, zm)
    for d in d_load(2, zp):
        d.start()
    out_compute(2, zp)
    finish(0, z)
    got(12, 13, 14)
    for d in d_load(3, zo):
        d.start()
    out_compute(3, zo)
    finish(1, zm)
    finish(2, zp)
    finish(3, zo)

    def drain(f, _):
        guc_sends(f)
        h_copy(f, c).wait_send()

        @pl.when(jnp.logical_not(home))
        def _():
            for h in PAIR:
                for m in PAIR:
                    nbr_copy(f, h, m).wait_send()
        return 0

    lax.fori_loop(0, NCH, drain, 0)
    for i in range(15):
        wdc(*SENT[i]).wait_send()
    for g in range(4):
        sent_all(g)

    @pl.when(home)
    def _():
        for m in PAIR:
            own_copy(m).wait_send()

    @pl.when(jnp.logical_or(jnp.logical_not(home), c == 1))
    def _():
        for i in PAIR:
            wd0_nbr(i).wait_send()


def solution(mesh):
    tok_spec = P(("rep", "expert", "data"), None)
    wide_spec = P("expert", "data", None)
    down_spec = P("expert", None, "data")
    dma = pltpu.SemaphoreType.DMA
    two, four, eight = dma((2,)), dma((4,)), dma((E,))
    hbm = pl.BlockSpec(memory_space=pltpu.HBM)
    vmem = pl.BlockSpec(memory_space=pltpu.VMEM)

    def device_step(x_loc, idx_loc, gate_loc, wg_loc, wu_loc, wd_loc):
        out = pl.pallas_call(
            kernel,
            out_shape=(jax.ShapeDtypeStruct((T, D), BF16),
                       jax.ShapeDtypeStruct((2, D, FH), BF16),
                       jax.ShapeDtypeStruct((4, 2, FF, 128), BF16),
                       jax.ShapeDtypeStruct((E, C, D), BF16)),
            in_specs=[vmem, vmem, vmem, hbm, hbm, hbm],
            out_specs=(vmem, hbm, hbm, hbm),
            scratch_shapes=[
                pltpu.VMEM((ROWS, D), BF16),
                pltpu.VMEM((ROWS, FF), BF16),
                pltpu.VMEM((2, 2, D, FC), BF16),
                pltpu.VMEM((2, FF, 256), BF16),
                pltpu.VMEM((E, C, D), BF16),
                pltpu.VMEM((T, 128), jnp.int32),
                pltpu.VMEM((T, 128), F32),
                two, two, dma((3,)),
                dma((NCH, 2)), dma((NCH, 2, 2)),
                dma((NCH, E)), dma((NCH, E)),
                two, two, dma((15,)), dma((15,)),
                eight, eight, eight, eight,
                dma((NCH,)), dma((NCH,)), two, dma((2, 2)),
                four, four, dma((1,)),
            ],
            compiler_params=pltpu.CompilerParams(has_side_effects=True, collective_id=0, vmem_limit_bytes=67043328),
        )(x_loc, idx_loc.T, gate_loc.T, wg_loc, wu_loc, wd_loc)
        return out[0]

    return jax.shard_map(device_step, mesh=mesh, in_specs=(tok_spec, tok_spec, tok_spec, wide_spec, wide_spec, down_spec), out_specs=tok_spec, check_vma=False)
```

time: 606 us -> 323 us (0.53)
  the two profiles are of different devices: /device:TPU:1 before, /device:TPU:55 now
where the time goes in v1:
time: 323 us
  Pallas kernels  319 us (99%)
    pallas_call x1, Pallas kernels, device_step(): pl.pallas_call(kernel, out_shape=(jax.ShapeDtypeStruct((T, D), BF16), jax...  319 us

profile of v1, /device:TPU:55, one launch (start us, length us, event | category | flops | bytes accessed | tf_op | source)
XLA Modules:
  0.0 322.6 jit_solution(5210948601590218282)
XLA Ops:
  0.0 319.4 %shard_map.64 = (bf16[512,2048]{1,0:T(8,128)(2,1)}, bf16[2,2048,2816]{2,1,0:T(8,128)(2,1)}, bf16[4,2,5632,128]{3,2,1,0:T(8,128)(2,1)}, bf16[8,160,2048]{2,1,0:T(8,128)(2,1)}) custom-call(bf16[512,2048]{1,0:T(8,128)(2,1)} %x_ref.1, s32[2,512]{1,0:T(2,128)} %bitcast.2, f32[2,512]{1,0:T(2,128)} %bitcast.3, bf16[1,128,5632]{2,1,0:T(8,128)(2,1)} %wg_ref.1, ...), custom_call_target="tpu_custom_call" | custom-call | tf_op jit(solution)/shard_map/pallas_call | solution.py:574
  319.4 3.2 copy.8

commit v2 on v1

--- a/solution.py
+++ b/solution.py
@@ -310,6 +310,16 @@
                     k = zz * 4 + l * 2 + o
                     n = ynat(e % 2, l, o)
                     S[e, :, k * 128:(k + 1) * 128] = r[:, n * 128:(n + 1) * 128]
+        if e == 0:
+            for m in PAIR:
+                own_copy(m).wait_recv()
+            stage1(0)
+            nbr_start(3)
+        if e == 3:
+            stage1(1)
+        if e == 6:
+            stage2(0)
+            nbr_start(4)
 
     def mine(b):
         return pl.ds(pl.multiple_of(b * C, C), C)
@@ -370,48 +380,42 @@
         pl.when(jnp.logical_and(i >= lo, i < hi))(fn)
 
     def tick(i, _):
-        @pl.when(i == 0)
-        def _():
-            for m in PAIR:
-                own_copy(m).wait_recv()
-
-        during(i, 0, NCH, lambda: stage1(i))
-        during(i, 0, E - 1, lambda: tok_copy((e_own + 1 + i) % E).start())
-        during(i, 0, NCH - 3, lambda: nbr_start(i + 3))
+        during(i, 2, NCH, lambda: stage1(i))
+        during(i, 2, NCH - 3, lambda: nbr_start(i + 3))
 
         @pl.when(jnp.logical_and(i == NCH - 3, jnp.logical_not(home)))
         def _():
             for k in PAIR:
                 wd0_nbr(k).start()
 
-        during(i, 2, NCH + 2, lambda: stage3(i - 2))
-        during(i, 1, NCH + 1, lambda: stage2(i - 1))
-
-        @pl.when(i == NCH)
+        during(i, 2, NCH + 1, lambda: stage2(i - 1))
+        during(i, 2, E - 1, lambda: tok_copy((e_own + 1 + i) % E).start())
+
+        @pl.when(i == NCH - 1)
         def _():
             wd0_nbr(0).wait_recv()
             put(0, 1, 2)
 
-        @pl.when(i == NCH + 1)
+        @pl.when(i == NCH)
         def _():
             wd0_nbr(1).wait_recv()
             put(3, 4, 5)
 
-        @pl.when(i == NCH + 2)
+        @pl.when(i == NCH + 1)
         def _():
             got(0)
             put(8, 10)
             got(1)
             put(9, 11)
 
-        @pl.when(i == NCH + 3)
+        @pl.when(i == NCH + 2)
         def _():
             got(3)
             put(6, 7)
 
         during(i, 4, NCH + 4, lambda: stage4(i - 4))
 
-        @pl.when(i == FIRST - 3)
+        @pl.when(i == FIRST - 1)
         def _():
             take_tokens(0)
 
@@ -425,10 +429,15 @@
             one_chunk(j)
             return 0
 
-        lax.fori_loop(done_by(i - 1), done_by(i), chunk, 0)
+        mid = jnp.minimum(done_by(i - 1) + 1, done_by(i))
+        lax.fori_loop(done_by(i - 1), mid, chunk, 0)
+        during(i, 2, NCH + 2, lambda: stage3(i - 2))
+        lax.fori_loop(mid, done_by(i), chunk, 0)
         return 0
 
-    lax.fori_loop(0, TICKS, tick, 0)
+    tok_copy((e_own + 1) % E).start()
+    tok_copy((e_own + 2) % E).start()
+    lax.fori_loop(2, TICKS, tick, 0)
     h_copy(NCH - 1, c).start()
 
     def d_load(g, zz):
@@ -462,17 +471,20 @@
         for d in d_load(g, zz):
             d.wait()
 
-        def tile(r, _):
-            rr = pl.ds(pl.multiple_of(r * MT, MT), MT)
+        def turn(k):
+            return (x + 1 + k) % NT
+
+        def tile(k, _):
+            rr = pl.ds(pl.multiple_of(turn(k) * MT, MT), MT)
             X[rr, g * 256:(g + 1) * 256] = jnp.dot(H[rr, :], dv[g % 2], preferred_element_type=F32).astype(BF16)
 
-            @pl.when(r > 0)
+            @pl.when(k > 0)
             def _():
-                out_send(g, zz, r - 1)
+                out_send(g, zz, turn(k - 1))
             return 0
 
         lax.fori_loop(0, NT, tile, 0)
-        out_send(g, zz, NT - 1)
+        out_send(g, zz, turn(NT - 1))
         pltpu.make_async_copy(X.at[mine(b_own), pl.ds(g * 256, 256)], back_ref.at[e_own, :, place(zz)], c_recv.at[g]).start()
 
     def got_all(g):

time: 323 us -> 296 us (0.916)
  the two profiles are of different devices: /device:TPU:55 before, /device:TPU:1 now
where the time goes in v2:
time: 296 us; the launch traced here: 295 us
  Pallas kernels  292 us (99%)
  local copies, waits for them, and re-layouts  3.16 us (1%)
    pallas_call x1, Pallas kernels, device_step(): pl.pallas_call(kernel, out_shape=(jax.ShapeDtypeStruct((T, D), BF16), jax...  292 us

profile of v2, /device:TPU:1, one launch (start us, length us, event | category | flops | bytes accessed | tf_op | source)
XLA Modules:
  0.0 295.2 jit_solution(12251688089536746752)
XLA Ops:
  0.0 292.0 %shard_map.64 = (bf16[512,2048]{1,0:T(8,128)(2,1)}, bf16[2,2048,2816]{2,1,0:T(8,128)(2,1)}, bf16[4,2,5632,128]{3,2,1,0:T(8,128)(2,1)}, bf16[8,160,2048]{2,1,0:T(8,128)(2,1)}) custom-call(bf16[512,2048]{1,0:T(8,128)(2,1)} %x_ref.1, s32[2,512]{1,0:T(2,128)} %bitcast.2, f32[2,512]{1,0:T(2,128)} %bitcast.3, bf16[1,128,5632]{2,1,0:T(8,128)(2,1)} %wg_ref.1, ...), custom_call_target="tpu_custom_call" | custom-call | tf_op jit(solution)/shard_map/pallas_call | solution.py:586
  292.0 3.2 %copy.8 = bf16[512,2048]{1,0:T(8,128)(2,1)} copy(bf16[512,2048]{1,0:T(8,128)(2,1)} %get-tuple-element.6) | data formatting | bytes 4194304

commit v3 on v2

--- a/solution.py
+++ b/solution.py
@@ -28,8 +28,11 @@
 TICKS = NCH + 4
 
 
+L = 128
+
+
 def al(v):
-    return pl.multiple_of(v, 128)
+    return pl.multiple_of(v, L)
 
 
 def ynat(s, yl, o):
@@ -86,7 +89,7 @@
     pl.semaphore_wait(barrier, 18)
 
     hx = pl.ds(al(c * FH), FH)
-    my_rows = pl.ds(al((z * 4 + yl * 2) * 128), 128)
+    my_rows = pl.ds(al((z * 4 + yl * 2) * L), L)
 
     def own_copy(m):
         src = (wg_ref, wu_ref)[m]
@@ -94,17 +97,17 @@
 
     def bounce_in(m):
         src = (wg_ref, wu_ref)[m]
-        return pltpu.make_async_copy(src.at[0, :, hx], H.at[pl.ds(m * 128, 128), hx], loc_sem.at[m])
+        return pltpu.make_async_copy(src.at[0, :, hx], H.at[pl.ds(m * L, L), hx], loc_sem.at[m])
 
     def bounce_out(m):
-        return pltpu.make_async_copy(H.at[pl.ds(m * 128, 128), hx], gu_ref.at[m, my_rows, :], own_sem.at[m])
+        return pltpu.make_async_copy(H.at[pl.ds(m * L, L), hx], gu_ref.at[m, my_rows, :], own_sem.at[m])
 
     def nbr_copy(f, h, m):
         src = (wg_ref, wu_ref)[m]
         cols = pl.ds(al(h * FH + f * FC), FC)
         dcols = pl.ds(al(f * FC), FC)
         nyl = (3 - y) % 2
-        rows = pl.ds(al((z * 4 + nyl * 2 + 1) * 128), 128)
+        rows = pl.ds(al((z * 4 + nyl * 2 + 1) * L), L)
         return remote(src.at[0, :, cols], gu_ref.at[m, rows, dcols], nbr_send.at[f, h, m], nbr_recv.at[f, m],
                       dict(data=qc, expert=2 * x + h))
 
@@ -129,9 +132,9 @@
 
     def wd0_loc(i):
         o, n = PARTS[i]
-        return pltpu.make_async_copy(dv.at[0, pl.ds(o, n), pl.ds(0, 128)], wdn_ref.at[z, yl, pl.ds(o, n), :], wd0_recv.at[i])
-
-    wd_in = pltpu.make_async_copy(wd_ref.at[0], dv.at[0, :, pl.ds(0, 128)], loc_sem.at[2])
+        return pltpu.make_async_copy(dv.at[0, pl.ds(o, n), pl.ds(0, L)], wdn_ref.at[z, yl, pl.ds(o, n), :], wd0_recv.at[i])
+
+    wd_in = pltpu.make_async_copy(wd_ref.at[0], dv.at[0, :, pl.ds(0, L)], loc_sem.at[2])
 
     @pl.when(home)
     def _():
@@ -162,7 +165,7 @@
         nbr_start(f)
 
     def rows(zz, l, o, n):
-        return pl.ds(al((zz * 4 + l * 2 + o) * 128), n * 128)
+        return pl.ds(al((zz * 4 + l * 2 + o) * L), n * L)
 
     def guc(f, r, i, dev):
         ref = gu_ref.at[:, r, pl.ds(al(f * FC), FC)]
@@ -272,7 +275,7 @@
         for i in ids:
             wdc(*GOT[i]).wait_recv()
 
-    lanes = lax.broadcasted_iota(jnp.int32, (T, 128), 1)
+    lanes = lax.broadcasted_iota(jnp.int32, (T, L), 1)
     ids = jnp.transpose(idx_ref[...])
     gates = jnp.transpose(gate_ref[...])
     i0 = ids[:, 0:1]
@@ -309,7 +312,7 @@
                 for o in PAIR:
                     k = zz * 4 + l * 2 + o
                     n = ynat(e % 2, l, o)
-                    S[e, :, k * 128:(k + 1) * 128] = r[:, n * 128:(n + 1) * 128]
+                    S[e, :, k * L:(k + 1) * L] = r[:, n * L:(n + 1) * L]
         if e == 0:
             for m in PAIR:
                 own_copy(m).wait_recv()
@@ -391,24 +394,24 @@
         during(i, 2, NCH + 1, lambda: stage2(i - 1))
         during(i, 2, E - 1, lambda: tok_copy((e_own + 1 + i) % E).start())
 
-        @pl.when(i == NCH - 1)
+        @pl.when(i == NCH)
         def _():
             wd0_nbr(0).wait_recv()
             put(0, 1, 2)
 
-        @pl.when(i == NCH)
+        @pl.when(i == NCH + 1)
         def _():
             wd0_nbr(1).wait_recv()
             put(3, 4, 5)
 
-        @pl.when(i == NCH + 1)
+        @pl.when(i == NCH + 2)
         def _():
             got(0)
             put(8, 10)
             got(1)
             put(9, 11)
 
-        @pl.when(i == NCH + 2)
+        @pl.when(i == NCH + 3)
         def _():
             got(3)
             put(6, 7)
@@ -440,35 +443,39 @@
     lax.fori_loop(2, TICKS, tick, 0)
     h_copy(NCH - 1, c).start()
 
-    def d_load(g, zz):
+    PAIRS = (((z, 0), (z, 1)), ((zm, yl), (zp, yl)), ((zm, 1 - yl), (zp, 1 - yl)), ((zo, 0), (zo, 1)))
+
+    def d_load(g):
         out = []
-        for l in PAIR:
-            lane = pl.ds(al(((l + c) % 2) * 128), 128)
-            out.append(pltpu.make_async_copy(wdn_ref.at[zz, l], dv.at[g % 2, :, lane], dl_sem.at[g % 2, l]))
+        for k, (zz, l) in enumerate(PAIRS[g]):
+            if g % 3:
+                lane = pl.ds(k * L, L)
+            else:
+                lane = pl.ds(al(((l + c) % 2) * L), L)
+            out.append(pltpu.make_async_copy(wdn_ref.at[zz, l], dv.at[g % 2, :, lane], dl_sem.at[g % 2, k]))
         return out
 
-    def place(zz):
+    def places(g):
+        if g % 3:
+            return [(k * L, al((zz * 4 + c * (3 - 2 * s - l) + (1 - c) * (2 * s + l)) * L), L)
+                    for k, (zz, l) in enumerate(PAIRS[g])]
         w = c * (1 - s) + (1 - c) * s
-        return pl.ds(al(zz * 512 + w * 256), 256)
-
-    def out_copy(g, zz, b):
-        xd = b // 4
-        cd = b % 2
-        od = (b // 2) % 2
-        yd = od * (3 - y) + (1 - od) * y
-        return remote(X.at[mine(b), pl.ds(g * 256, 256)], back_ref.at[e_own, :, place(zz)],
-                      c_send.at[g], c_recv.at[g], dict(data=z * 4 + yd, expert=2 * xd + cd))
-
-    def out_send(g, zz, r):
+        return [(0, al(PAIRS[g][0][0] * 512 + w * FC), FC)]
+
+    def out_send(g, r):
         for k in range(4):
             b = r * 4 + k
+            od = k // 2
+            yd = 3 - y if od else y
 
             @pl.when(b != b_own)
             def _():
-                out_copy(g, zz, b).start()
-
-    def out_compute(g, zz):
-        for d in d_load(g, zz):
+                for lane, dst, n in places(g):
+                    remote(X.at[mine(b), pl.ds(g * 256 + lane, n)], back_ref.at[e_own, :, pl.ds(dst, n)],
+                           c_send.at[g], c_recv.at[g], dict(data=z * 4 + yd, expert=2 * r + k % 2)).start()
+
+    def out_compute(g):
+        for d in d_load(g):
             d.wait()
 
         def turn(k):
@@ -480,12 +487,13 @@
 
             @pl.when(k > 0)
             def _():
-                out_send(g, zz, turn(k - 1))
+                out_send(g, turn(k - 1))
             return 0
 
         lax.fori_loop(0, NT, tile, 0)
-        out_send(g, zz, turn(NT - 1))
-        pltpu.make_async_copy(X.at[mine(b_own), pl.ds(g * 256, 256)], back_ref.at[e_own, :, place(zz)], c_recv.at[g]).start()
+        out_send(g, turn(NT - 1))
+        for lane, dst, n in places(g):
+            pltpu.make_async_copy(X.at[mine(b_own), pl.ds(g * 256 + lane, n)], back_ref.at[e_own, :, pl.ds(dst, n)], c_recv.at[g]).start()
 
     def got_all(g):
         pltpu.make_async_copy(X.at[:, pl.ds(0, 256)], X.at[:, pl.ds(0, 256)], c_recv.at[g]).wait()
@@ -493,8 +501,7 @@
     def sent_all(g):
         pltpu.make_async_copy(X.at[pl.ds(0, 15 * C), pl.ds(0, 256)], X.at[pl.ds(0, 15 * C), pl.ds(0, 256)], c_send.at[g]).wait()
 
-    def finish(g, zz):
-        got_all(g)
+    def finish(zz):
         cols = pl.ds(al(zz * 512), 512)
         back = pltpu.make_async_copy(back_ref.at[:, :, cols], S.at[:, :, cols], bl_sem.at[0])
         back.start()
@@ -519,31 +526,38 @@
             tok_copy(e).wait_send()
 
     got(2)
-    for d in d_load(0, z):
+    for d in d_load(0):
         d.start()
     for f in range(NCH):
         h_copy(f, 1 - c).wait_recv()
-    out_compute(0, z)
+    out_compute(0)
     got(8, 9)
     put(14)
-    got(4, 5, 6, 7)
-    put(12, 13)
-    got(10)
-    for d in d_load(1, zm):
+    got(4, 5)
+    for d in d_load(1):
         d.start()
-    got(11)
-    out_compute(1, zm)
-    for d in d_load(2, zp):
+    pl.when(yl == 0)(lambda: put(12))
+    pl.when(yl == 1)(lambda: put(13))
+    out_compute(1)
+    got(6, 7)
+    pl.when(yl == 1)(lambda: put(12))
+    pl.when(yl == 0)(lambda: put(13))
+    got(10, 11)
+    for d in d_load(2):
         d.start()
-    out_compute(2, zp)
-    finish(0, z)
+    out_compute(2)
+    got_all(0)
+    finish(z)
     got(12, 13, 14)
-    for d in d_load(3, zo):
+    for d in d_load(3):
         d.start()
-    out_compute(3, zo)
-    finish(1, zm)
-    finish(2, zp)
-    finish(3, zo)
+    out_compute(3)
+    got_all(1)
+    got_all(2)
+    finish(zm)
+    finish(zp)
+    got_all(3)
+    finish(zo)
 
     def drain(f, _):
         guc_sends(f)
@@ -587,7 +601,7 @@
             kernel,
             out_shape=(jax.ShapeDtypeStruct((T, D), BF16),
                        jax.ShapeDtypeStruct((2, D, FH), BF16),
-                       jax.ShapeDtypeStruct((4, 2, FF, 128), BF16),
+                       jax.ShapeDtypeStruct((4, 2, FF, L), BF16),
                        jax.ShapeDtypeStruct((E, C, D), BF16)),
             in_specs=[vmem, vmem, vmem, hbm, hbm, hbm],
             out_specs=(vmem, hbm, hbm, hbm),
@@ -597,8 +611,8 @@
                 pltpu.VMEM((2, 2, D, FC), BF16),
                 pltpu.VMEM((2, FF, 256), BF16),
                 pltpu.VMEM((E, C, D), BF16),
-                pltpu.VMEM((T, 128), jnp.int32),
-                pltpu.VMEM((T, 128), F32),
+                pltpu.VMEM((T, L), jnp.int32),
+                pltpu.VMEM((T, L), F32),
                 two, two, dma((3,)),
                 dma((NCH, 2)), dma((NCH, 2, 2)),
                 dma((NCH, E)), dma((NCH, E)),

time: 296 us -> 292 us (0.986); the launches traced: 295 us -> 288 us
  Pallas kernels: 292 us -> 285 us
    pallas_call x1, Pallas kernels: 292 us -> 285 us  [device_step(): pl.pallas_call(kernel, out_shape=(jax.ShapeDtypeStruct((T, D), BF16), jax...]
where the time goes in v3:
time: 292 us; the launch traced here: 288 us
  Pallas kernels  285 us (98%)
  local copies, waits for them, and re-layouts  3.16 us (1%)
    pallas_call x1, Pallas kernels, device_step(): pl.pallas_call(kernel, out_shape=(jax.ShapeDtypeStruct((T, D), BF16), jax...  285 us

profile of v3, /device:TPU:1, one launch (start us, length us, event | category | flops | bytes accessed | tf_op | source)
XLA Modules:
  0.0 288.1 jit_solution(10269652500161757592)
XLA Ops:
  0.0 284.9 %shard_map.64 = (bf16[512,2048]{1,0:T(8,128)(2,1)}, bf16[2,2048,2816]{2,1,0:T(8,128)(2,1)}, bf16[4,2,5632,128]{3,2,1,0:T(8,128)(2,1)}, bf16[8,160,2048]{2,1,0:T(8,128)(2,1)}) custom-call(bf16[512,2048]{1,0:T(8,128)(2,1)} %x_ref.1, s32[2,512]{1,0:T(2,128)} %bitcast.2, f32[2,512]{1,0:T(2,128)} %bitcast.3, bf16[1,128,5632]{2,1,0:T(8,128)(2,1)} %wg_ref.1, ...), custom_call_target="tpu_custom_call" | custom-call | tf_op jit(solution)/shard_map/pallas_call | solution.py:600
  284.9 3.2 %copy.8 = bf16[512,2048]{1,0:T(8,128)(2,1)} copy(bf16[512,2048]{1,0:T(8,128)(2,1)} %get-tuple-element.6) | data formatting | bytes 4194304
